TPU v7x, 16 devices: a whole 2x2x2 slice. The times are simulated.
16 devices in a mesh: graph: 16 (over z, y, x, core).
Axes of the slice: x: 2, y: 2, z: 2, core: 2. Of those that a mesh axis runs over, the one named last changes fastest.
Arguments:
- node_feats: bfloat16 [32768, 128], P('graph')
- w_one: float32 [128, 256], replicated
- w_two: float32 [256, 172], replicated
- send_idx: int32 [32, 1024], P('graph')
- edge_src: int32 [131072], P('graph')
- edge_dst: int32 [131072], P('graph')
- edge_w: float32 [131072], P('graph')
- labels: int32 [32768], P('graph')
- label_mask: int32 [32768], P('graph')
Outputs:
- output 1: float32 [], replicated
- output 2: float32 [128, 256], replicated
- output 3: float32 [256, 172], replicated
All inputs are finite; a program needn't handle non-finite values.
Results may differ from a plain program's by a relative error of at most 0.001.
Values are sent between devices in bfloat16 or wider.
A program may use at most 1 GiB of HBM per device.

v0:
```python
import functools

import jax
import jax.numpy as jnp
from jax import lax
from jax.experimental import pallas as pl
from jax.experimental.pallas import tpu as pltpu
from jax.sharding import PartitionSpec as P

AXIS = "graph"
LANES = 128
ROWS_A = (((0,), (0,)), ((), ()))
COLS_A = (((1,), (1,)), ((), ()))
F32, BF16 = jnp.float32, jnp.bfloat16
VMEM = pl.BlockSpec(memory_space=pltpu.VMEM)
SMEM = pl.BlockSpec(memory_space=pltpu.SMEM)
ANY = pl.BlockSpec(memory_space=pl.ANY)
STEP = 512
BLOCK = 256
BYTE = BLOCK
SUB = 8
TILE = (SUB, LANES)
SQUARE = (LANES, LANES)
PREP_CHUNK = 64
SMALL = PREP_CHUNK
SEGMENT = 1024
MESH = pl.DeviceIdType.MESH


def dot(a, b, dims=(((1,), (0,)), ((), ()))):
    return lax.dot_general(a, b, dims, preferred_element_type=F32)


def fill_zero(ref):
    step = BLOCK if ref.shape[0] % BLOCK == 0 else SMALL
    zero = jnp.zeros((step, LANES), F32)

    @pl.loop(0, ref.shape[0], step=step)
    def _(i):
        ref[pl.ds(i, step), :] = zero


def copy_in(dst, src):
    @pl.loop(0, dst.shape[0], step=STEP)
    def _(i):
        dst[pl.ds(i, STEP), :] = src[pl.ds(i, STEP), :].astype(F32)


class Edges:
    def __init__(self, first, last, w, arrays, smem, sems):
        self.first, self.last, self.w = first, last, w
        self.pairs = tuple(zip(arrays, smem))
        self.sems = sems

    def copies(self, seg):
        part = pl.ds(pl.multiple_of(seg * SEGMENT, SEGMENT), SEGMENT)
        return [pltpu.make_async_copy(a.at[part], b.at[part], self.sems.at[i, seg]) for i, (a, b) in enumerate(self.pairs)]

    def fetch(self):
        per = SEGMENT // PREP_CHUNK
        for seg in range(self.pairs[0][1].shape[0] // SEGMENT):

            @pl.when(jnp.logical_and(seg * per < self.last, (seg + 1) * per > self.first))
            def _():
                for c in self.copies(seg):
                    c.start()

    def walk(self, chunk, from_idx, to_idx, table, accs, wait):
        group, per, ratio = len(accs), SEGMENT // chunk, PREP_CHUNK // chunk
        first, last = self.first * ratio, self.last * ratio

        def body(c, _):
            base = c * chunk
            w_chunk = self.w.at[pl.ds(pl.multiple_of(base, chunk), chunk)]
            for g in range(0, chunk, group):
                pend = []
                for u in range(group):
                    k = base + g + u
                    s = pl.multiple_of(from_idx[k], 2)
                    d = pl.multiple_of(to_idx[k], 2)
                    pend.append((d, accs[u][pl.ds(d, 2), :] + table[pl.ds(s, 2), :] * w_chunk[g + u : g + u + 1, :]))
                for u in range(group):
                    accs[u][pl.ds(pend[u][0], 2), :] = pend[u][1]
            return 0

        if not wait:
            lax.fori_loop(first, last, body, 0)
            return

        def segment(seg, _):
            for c in self.copies(seg):
                c.wait()
            lax.fori_loop(jnp.maximum(first, seg * per), jnp.minimum(last, (seg + 1) * per), body, 0)
            return 0

        lax.fori_loop(first // per, (last + per - 1) // per, segment, 0)


def one_hot_rows(idx, which, start, table):
    lane = across(SQUARE)
    hot = []
    for q in range(2):
        want = spread(idx[which : which + 1, pl.ds(pl.multiple_of(start + q * LANES, LANES), LANES)])
        hot.append(
            stack_lanes([jnp.where(want == lane + LANES * j, 1.0, 0.0).astype(BF16) for j in range(table.shape[0] // LANES)])
        )
    return dot(stack_rows(hot), table[...])


def low_lanes(rows):
    return across((rows, LANES)) < LANES // 2


def swap_lanes(v):
    return pltpu.roll(v, LANES // 2, 1)


def fetch_index(send, idx, sems):
    parts = [pl.ds(i, LANES) for i in range(0, send.shape[1], LANES)]
    return [pltpu.make_async_copy(send.at[1, p], idx.at[p], sems.at[i]) for i, p in enumerate(parts)]


def gather_block(send, idx, i, table_b, table, buf):
    got = one_hot_rows(send, 0, i, table_b)
    out = buf.at[pl.ds(pl.multiple_of(2 * i, 512), 512)]
    for u in range(BLOCK):
        s = pl.multiple_of(idx[i + u] * 2, 2)
        out[2 * u : 2 * u + 2, :] = table[pl.ds(s, 2), :]
    return got


def gather_rows(send, idx, table_b, table, buf, to_prev, to_next, also):
    @pl.loop(0, to_prev.shape[0], step=BLOCK)
    def _(i):
        i = pl.multiple_of(i, BLOCK)
        to_prev[pl.ds(i, BLOCK), :] = gather_block(send, idx, i, table_b, table, buf).astype(BF16)
        also(i)

    @pl.loop(0, to_next.shape[0], step=BLOCK)
    def _(i):
        to_next[pl.ds(pl.multiple_of(i, BLOCK), BLOCK), :] = stack_lanes(halves([buf], i, BLOCK)).astype(BF16)


def pack_rows(out, i, half, a_even, a_odd, b_even, b_odd):
    n = a_even.shape[0]
    out[pl.ds(i, n), :] = a_even.astype(out.dtype)
    out[pl.ds(half + i, n), :] = b_even.astype(out.dtype)
    out[pl.ds(2 * half + i, n), :] = jnp.where(low_lanes(n), a_odd, swap_lanes(b_odd)).astype(out.dtype)


def gather_packed(send, idx, table_b, table, buf, to_prev, to_next):
    half = to_prev.shape[0] // 3

    @pl.loop(0, half, step=BLOCK)
    def _(i):
        i = pl.multiple_of(i, BLOCK)
        a = gather_block(send, idx, i, table_b, table, buf)
        b = gather_block(send, idx, half + i, table_b, table, buf)
        pack_rows(to_prev, i, half, a[:, :LANES], a[:, LANES:], b[:, :LANES], b[:, LANES:])

    @pl.loop(0, half, step=BLOCK)
    def _(i):
        i = pl.multiple_of(i, BLOCK)
        pack_rows(to_next, i, half, *halves([buf], i, BLOCK), *halves([buf], half + i, BLOCK))


def unpack_rows(got, table, start, half=None):
    half = got.shape[0] // 3 if half is None else half
    n = half // 2

    @pl.loop(0, half, step=n)
    def _(i):
        i = pl.multiple_of(i, n)
        a, b, both = (got[pl.ds(k + i, n), :].astype(F32) for k in (0, half, 2 * half))
        put_halves(table, start + i, n, a, jnp.where(low_lanes(n), both, 0.0))
        put_halves(table, start + half + i, n, b, jnp.where(low_lanes(n), swap_lanes(both), 0.0))


def unpack_plain(got, table, start):
    @pl.loop(0, got.shape[0], step=BLOCK)
    def _(i):
        t = got[pl.ds(i, BLOCK), :].astype(F32)
        put_halves(table, start + i, BLOCK, t[:, :LANES], t[:, LANES:])


def spread(row):
    return jnp.transpose(jnp.broadcast_to(row, SQUARE))


def return_rows(back, slots, start, count, vals, accs, chunk=32):
    group = len(accs)

    def body(c, _):
        block = vals.at[pl.ds(pl.multiple_of(c * 2 * chunk, 2 * chunk), 2 * chunk)]
        for g in range(0, chunk, group):
            pend = []
            for u in range(group):
                d = pl.multiple_of(back[slots[start + c * chunk + g + u]], 2)
                pend.append((d, accs[u][pl.ds(d, 2), :] + block[2 * (g + u) : 2 * (g + u) + 2, :]))
            for u in range(group):
                accs[u][pl.ds(pend[u][0], 2), :] = pend[u][1]
        return 0

    lax.fori_loop(0, (count + chunk - 1) // chunk, body, 0)


def group(i, n, which):
    return pl.ds(2 * i + which, n, stride=2), slice(None)


def halves(accs, i, n):
    return [functools.reduce(jnp.add, [a[group(i, n, k)] for a in accs]) for k in range(2)]


def put_halves(table, i, n, *parts):
    for k, part in enumerate(parts):
        table[group(i, n, k)] = part


def stack_rows(parts):
    return jnp.concatenate(parts, axis=0)


def stack_lanes(parts):
    return jnp.concatenate(parts, axis=1)


def down(shape):
    return lax.broadcasted_iota(jnp.int32, shape, 0)


def across(shape):
    return lax.broadcasted_iota(jnp.int32, shape, 1)


def prefix(mask, above):
    m = mask.astype(BF16)
    before = (down(SQUARE) < across(SQUARE)).astype(BF16)
    return dot(m, before) + dot(above, dot(m, jnp.ones(SQUARE, BF16)).astype(BF16))


def rank_halo(halo, counts, src, used, src_back, lists):
    lines = used.shape[0]
    side = lines // 2
    i, j = down((lines, lines)), across((lines, lines))
    above = jnp.logical_and(j < i, (j >= side) == (i >= side)).astype(F32).astype(BF16)
    rank = prefix(used[...], above).astype(jnp.int32)
    low, high = rank & (LANES - 1), rank >> 7
    table = stack_rows([low.astype(F32), high.astype(F32)]).astype(BF16)

    quad = 4

    def four(c, _):
        slot = [src[pl.ds(c * quad + q, 1), :] >> 1 for q in range(quad)]
        spots = stack_lanes([(down(SQUARE) == (t & (LANES - 1))).astype(F32) for t in slot]).astype(BF16)
        got = dot(table, spots)
        h = stack_lanes(slot) >> 7
        got = jnp.where(down(got[:lines].shape) == h, got[:lines] + LANES * got[lines:], 0.0)
        got = (jnp.sum(got, axis=0, keepdims=True).astype(jnp.int32) + jnp.where(h >= side, halo, 0)) * 2
        for q in range(quad):
            src_back[pl.ds(c * quad + q, 1), :] = got[:, q * LANES : (q + 1) * LANES]
        return 0

    ratio = quad * LANES // PREP_CHUNK
    lax.fori_loop(counts[0] // ratio, (counts[1] + ratio - 1) // ratio, four, 0)
    for k in range(2):
        acc = jnp.zeros((24, LANES), F32)
        for hh in range(side):
            q = k * side + hh
            pick = jnp.where(down(TILE) == high[q : q + 1, :], used[q : q + 1, :], 0.0)
            lhs = stack_rows([pick * across(TILE).astype(F32), pick * hh, pick]).astype(BF16)
            acc += dot(lhs, (down(SQUARE) == low[q : q + 1, :]).astype(F32).astype(BF16), COLS_A)
        slots = acc[:8] + LANES * acc[8:16]
        lists[k * side : (k + 1) * side, :] = jnp.where(acc[16:24] > 0.0, slots[:side], -1.0)


def first_kernel(compact, halo, tab, tab_b, send, counts, src, w, used, to_prev, to_next, w_out, src_back, lists, buf, idx, sems):
    fetch = fetch_index(send, idx, sems)
    for c in fetch:
        c.start()
    src_back[...] = src[...]
    if compact:
        rank_halo(halo, counts, src, used, src_back, lists)
    else:
        line = down(lists.shape)
        line = jnp.where(line >= lists.shape[0] // 2, line - lists.shape[0] // 2, line)
        lists[...] = (line * LANES + across(lists.shape)).astype(F32)
    for c in fetch:
        c.wait()
    share = w.shape[0] * BLOCK // halo

    def widen(i):
        for q in range(share):
            r = i // BLOCK * share + q
            w_out[pl.ds(pl.multiple_of(r * LANES, LANES), LANES), :] = spread(w[pl.ds(r, 1), :])

    gather_rows(send, idx, tab_b, tab, buf, to_prev, to_next, widen)


def greet(n):
    me = lax.axis_index(AXIS)
    barrier = pltpu.get_barrier_semaphore()
    for o in range(1, n):
        pl.semaphore_signal(barrier, inc=1, device_id=(lax.rem(me + o, n),), device_id_type=MESH)
    return me, lambda: pl.semaphore_wait(barrier, n - 1)


def remote(src, dst, send_sem, recv_sem, peer):
    return pltpu.make_async_remote_copy(
        src_ref=src, dst_ref=dst, send_sem=send_sem, recv_sem=recv_sem, device_id=(peer,), device_id_type=MESH
    )


def reduce_kernel(n, one, two, loss, count, one_out, two_out, mean, work, full, got_pair, got_rest, sems):
    me = lax.axis_index(AXIS)
    chips, core = n // 2, lax.rem(me, 2)
    chip = lax.div(me, 2)
    pair = me + 1 - 2 * core
    others = [lax.rem(chip + o, chips) for o in range(1, chips)]
    barrier = pltpu.get_barrier_semaphore()
    for p in [pair] + [2 * c + core for c in others]:
        pl.semaphore_signal(barrier, inc=1, device_id=(p,), device_id_type=MESH)
    classes = two_out.shape[0]
    lines = -(-classes // SUB) * SUB
    top, wide = one.shape
    work[:top, :] = one[:, :LANES]
    work[top : 2 * top, :] = one[:, LANES:]
    work[2 * top : 2 * top + lines, :] = two[:lines, :LANES]
    work[2 * top + lines : 2 * top + 2 * lines, :] = two[:lines, LANES:]
    tail = 2 * top + 2 * lines
    work[tail : tail + SUB, :] = loss[...]
    work[tail + SUB :, :] = jnp.zeros((work.shape[0] - tail - SUB, LANES), F32)
    pl.semaphore_wait(barrier, chips)

    half = work.shape[0] // 2
    piece = half // chips
    spot = lambda c, k: pl.ds(pl.multiple_of(k * half + c * piece, SUB), piece)
    link = lambda kind, o, src, dst, peer: remote(src, dst, sems.at[0, kind * chips + o], sems.at[1, kind * chips + o], peer)
    order = list(enumerate(others + [chip]))
    swap = [link(0, o, work.at[spot(c, 1 - core)], got_pair.at[pl.ds(o * piece, piece)], pair) for o, c in order]
    for c in swap:
        c.start()
    scatter = [link(1, o, work.at[spot(c, core)], got_rest.at[o], 2 * c + core) for o, c in order[:-1]]
    for o, c in order:
        swap[o].wait_recv()
        work[spot(c, core), :] += got_pair[o * piece : (o + 1) * piece, :]
        if o:
            scatter[o - 1].start()
    for c in scatter:
        c.wait_recv()
    own = spot(chip, core)
    work[own, :] += jnp.sum(got_rest[...], axis=0)
    full[own, :] = work[own, :]
    for c in swap + scatter:
        c.wait_send()
    gather = [link(2, o, work.at[own], full.at[own], 2 * c + core) for o, c in order[:-1]]
    for c in gather:
        c.start()
    forward = [link(3, chips - 1, work.at[own], full.at[own], pair)]
    forward[0].start()
    for o, _ in order[:-1]:
        gather[o].wait_recv()
        came = spot(lax.rem(chip + chips - 1 - o, chips), core)
        forward.append(link(3, o, full.at[came], full.at[came], pair))
        forward[-1].start()
    for c in gather:
        c.wait_send()
    for c in forward:
        c.wait()
    one_out[:, :LANES] = full[:top, :]
    one_out[:, LANES:] = full[top : 2 * top, :]
    two_out[:, :LANES] = full[2 * top : 2 * top + classes, :]
    two_out[:, LANES:] = full[2 * top + lines : 2 * top + lines + classes, :]
    mean[...] = jnp.sum(full[tail : tail + SUB, :], keepdims=True) / count[:1, :1]


def prep_kernel(n, chunk, rows, src_in, dst_in, w_in, mask, x, w1, tab, tab_b, src_out, dst_out, w_out, used, counts, count, need, total, values, places, hits, mine, theirs, send_sem, recv_sem):
    me, met = greet(n)
    lines, slots = src_in.shape[0], src_out.shape[0]
    src, d, half_w = src_in[...], dst_in[...], w_in[...] * 0.5
    live = w_in[...] != 0.0
    halo = src >= rows
    above = (across((lines, lines)) < down((lines, lines))).astype(F32).astype(BF16)
    is_local, is_halo = jnp.logical_and(live, jnp.logical_not(halo)), jnp.logical_and(live, halo)
    rank = lambda m: prefix(m.astype(F32), above).astype(jnp.int32)
    n_local = jnp.sum(is_local.astype(F32)).astype(jnp.int32)
    n_halo = jnp.sum(is_halo.astype(F32)).astype(jnp.int32)
    local_chunks = (n_local + chunk - 1) // chunk
    counts[0] = local_chunks
    counts[1] = local_chunks + (n_halo + chunk - 1) // chunk
    pos = jnp.where(is_local, rank(is_local), jnp.where(is_halo, rank(is_halo) + local_chunks * chunk, -1))
    s = jnp.where(halo, src - rows, src)
    w_a = half_w.astype(BF16).astype(F32)
    w_b = (half_w - w_a).astype(BF16).astype(F32)
    w_c = half_w - w_a - w_b
    high = ((s >> 8) * 8 + (d >> 8)).astype(F32)
    planes = [(s % BYTE).astype(F32), (d % BYTE).astype(F32), high, w_a, w_b, w_c]
    for i, p in enumerate(planes):
        values[i * lines : (i + 1) * lines, :] = p
    for i, p in enumerate((pos >> 7, pos & (LANES - 1), jnp.where(is_halo, s >> 7, -1), s & (LANES - 1))):
        places[i * lines : (i + 1) * lines, :] = p
    row = lambda i, q: pl.ds(i * lines + q, 1)
    spot = lambda size, i, q: (down((size, LANES)) == places[row(i, q), :]).astype(F32)
    hits[...] = jnp.zeros_like(hits)

    @pl.loop(0, lines, step=SUB)
    def _(base):
        acc = None
        for r in range(0, SUB, 2):
            lhs = stack_lanes([spot(hits.shape[0], 2, base + q) for q in (r, r + 1)]).astype(BF16)
            rhs = stack_lanes([spot(LANES, 3, base + q) for q in (r, r + 1)]).astype(BF16)
            part = dot(lhs, rhs, COLS_A)
            acc = part if acc is None else acc + part
        hits[...] += acc

    flags = (hits[...] > 0.0).astype(F32)
    used[...] = flags
    side = hits.shape[0] // 2
    most = jnp.maximum(jnp.sum(flags[:side], keepdims=True), jnp.sum(flags[side:], keepdims=True))
    mine[:1, :] = jnp.sum(mask[...].astype(F32), axis=0, keepdims=True)
    mine[1:, :] = jnp.broadcast_to(most, (1, LANES))
    met()
    copies = [remote(mine, theirs.at[o - 1], send_sem.at[o - 1], recv_sem.at[o - 1], lax.rem(me + o, n)) for o in range(1, n)]
    for c in copies:
        c.start()
    total[...] = jnp.zeros_like(total)

    @pl.loop(0, lines, step=SUB)
    def _(base):
        acc = None
        for r in range(0, SUB, 2):
            lhs, rhs = [], []
            for q in (base + r, base + r + 1):
                pick = down((slots, LANES)) == places[row(0, q), :]
                lhs.append(stack_rows([jnp.where(pick, values[row(i, q), :], 0.0) for i in range(len(planes))]))
                rhs.append(spot(LANES, 1, q))
            part = dot(stack_lanes(lhs).astype(BF16), stack_lanes(rhs).astype(BF16), COLS_A)
            acc = part if acc is None else acc + part
        total[...] += acc

    plane = lambda i: total[i * slots : (i + 1) * slots, :]
    high = plane(2).astype(jnp.int32)
    w1_b = w1[...].astype(BF16)

    @pl.loop(0, rows, step=STEP)
    def _(i):
        t = dot(x[pl.ds(i, STEP), :], w1_b).astype(BF16)
        tab_b[pl.ds(i, STEP), :] = t
        t = t.astype(F32)
        put_halves(tab, i, STEP, t[:, :LANES], t[:, LANES:])

    src_out[...] = ((high >> 3) * BYTE + plane(0).astype(jnp.int32)) * 2
    dst_out[...] = ((high & 7) * BYTE + plane(1).astype(jnp.int32)) * 2
    w_out[...] = (plane(3) + plane(4) + plane(5)) * 2.0
    for c in copies:
        c.wait()
    every = jnp.sum(mine[:1, :] + jnp.sum(theirs[:, :1, :], axis=0), keepdims=True)
    count[...] = jnp.maximum(jnp.broadcast_to(every, count.shape), 1.0)
    need[0] = jnp.max(jnp.maximum(mine[1:, :], jnp.max(theirs[:, 1:, :], axis=0))).astype(jnp.int32)


def local_kernel(chunk, backward, counts, src, dst, w, table, out, src_s, dst_s, sems, *accs):
    edges = Edges(0, counts[0], w, (src, dst), (src_s, dst_s), sems)
    edges.fetch()
    for a in accs:
        fill_zero(a)
    edges.walk(chunk, *((dst_s, src_s) if backward else (src_s, dst_s)), table, accs, True)

    @pl.loop(0, out.shape[0], step=STEP)
    def _(i):
        out[pl.ds(i, STEP), :] = functools.reduce(jnp.add, [a[pl.ds(i, STEP), :] for a in accs])


def forward_halo(chunk, edges, src_s, dst_s, from_prev, from_next, part, htab, accs, unpack):
    edges.fetch()
    unpack(from_prev, htab, 0)
    unpack(from_next, htab, htab.shape[0] // 4)
    copy_in(accs[0], part)
    for a in accs[1:]:
        fill_zero(a)
    edges.walk(chunk, src_s, dst_s, htab, accs, True)


def backward_halo(limit, chunk, edges, src_s, dst_s, grad, back_prev, back_next, accs, wait, lists=None):
    split = accs[0].shape[0] // 2
    for a in accs:
        for start in (0, split):
            fill_zero(a.at[pl.ds(start, limit * 2)])
    edges.walk(chunk, dst_s, src_s, grad, accs, wait)
    if lists is None:

        @pl.loop(0, back_prev.shape[0], step=SMALL)
        def _(i):
            back_prev[pl.ds(i, SMALL), :] = functools.reduce(jnp.add, [a[pl.ds(i, SMALL), :] for a in accs])
            back_next[pl.ds(i, SMALL), :] = functools.reduce(jnp.add, [a[pl.ds(split + i, SMALL), :] for a in accs])
        return
    side = lists.shape[0] // 2
    half = (back_prev.shape[0] - side) // 3
    n = half // 2
    for k, out in enumerate((back_prev, back_next)):
        start = k * (split // 2)

        @pl.loop(0, half, step=n)
        def _(i):
            i = pl.multiple_of(i, n)
            pack_rows(out, i, half, *halves(accs, start + i, n), *halves(accs, start + half + i, n))

        out[3 * half : 3 * half + side, :] = lists[k * side : (k + 1) * side, :]


def padded(w, buf):
    low = w.shape[0] // SUB * SUB
    buf[low:, :] = jnp.zeros((buf.shape[0] - low, buf.shape[1]), F32)
    buf[:w.shape[0], :] = w[...]
    return buf[...].astype(BF16)


def hidden_kernel(chunk, counts, src, dst, w, send, from_prev, from_next, part, w2, hid, tab, to_prev, to_next, back, htab, tab_b, w2_pad, buf, idx, idx_sems, src_s, dst_s, sems, *accs):
    fetch = fetch_index(send, idx, idx_sems)
    for c in fetch:
        c.start()
    edges = Edges(counts[0], counts[1], w, (src, dst), (src_s, dst_s), sems)
    w2_b = padded(w2, w2_pad)
    per = send.shape[1] // LANES
    for i in range(2 * per):
        back[i : i + 1, :] = send[i // per : i // per + 1, (i % per) * LANES : (i % per + 1) * LANES] * 2
    forward_halo(chunk, edges, src_s, dst_s, from_prev, from_next, part, htab, accs, unpack_plain)

    @pl.loop(0, hid.shape[0], step=STEP)
    def _(i):
        even, odd = halves(accs, i, STEP)
        h = stack_lanes([jnp.maximum(even, 0.0), jnp.maximum(odd, 0.0)]).astype(BF16)
        hid[pl.ds(i, STEP), :] = h
        t = dot(h, w2_b, COLS_A).astype(BF16)
        tab_b[pl.ds(i, STEP), :] = t
        t = t.astype(F32)
        put_halves(tab, i, STEP, t[:, :LANES], t[:, LANES:])

    for c in fetch:
        c.wait()
    gather_packed(send, idx, tab_b, tab, buf, to_prev, to_next)


def loss_kernel(limit, quad, chunk, classes, counts, src, dst, w, src_back, lists, count, from_prev, from_next, part, labels, mask, loss, grad, back_prev, back_next, htab, src_s, dst_s, back_s, sems, *accs):
    edges = Edges(counts[0], counts[1], w, (src, dst, src_back), (src_s, dst_s, back_s), sems)
    forward_halo(chunk, edges, src_s, dst_s, from_prev, from_next, part, htab, accs, unpack_rows)
    lane = across(SQUARE)
    live = lane < classes - LANES
    scale = 1.0 / count[:1, :]
    loss[...] = jnp.zeros_like(loss)

    @pl.loop(0, labels.shape[0], step=quad)
    def _(first):
        for b in [first + q for q in range(quad)]:
            even, odd = halves(accs, b * LANES, LANES)
            odd = jnp.where(live, odd, -jnp.inf)
            keep = spread(mask[pl.ds(b, 1), :])
            label = jnp.where(keep > 0, spread(labels[pl.ds(b, 1), :]), -1)
            hit_even, hit_odd = lane == label, lane + LANES == label
            top = jnp.max(jnp.maximum(even, odd), axis=1, keepdims=True)
            exp_even, exp_odd = jnp.exp(even - top), jnp.exp(odd - top)
            total = jnp.sum(exp_even + exp_odd, axis=1, keepdims=True)
            norm = jnp.where(jnp.logical_and(lane == 0, keep > 0), top + jnp.log(total), 0.0)
            per_row = norm - jnp.where(hit_even, even, jnp.where(hit_odd, odd, 0.0))
            loss[...] += jnp.sum(per_row.reshape(LANES // SUB, *TILE), axis=0)
            share = keep.astype(F32) * scale * (1.0 / total)
            put_halves(
                grad, b * LANES, LANES, *(e * share - jnp.where(hit, scale, 0.0) for e, hit in ((exp_even, hit_even), (exp_odd, hit_odd)))
            )

    backward_halo(limit, chunk, edges, back_s, dst_s, grad, back_prev, back_next, accs, False, lists)


def take_returns(back, slots, counts, part, got_prev, got_next, accs):
    return_rows(back, slots, 0, counts[0], got_prev, accs)
    return_rows(back, slots, slots.shape[0] // 2, counts[1], got_next, accs)


def fetch_lines(lines, smem, sems):
    return [pltpu.make_async_copy(lines.at[i], smem.at[pl.ds(i * LANES, LANES)], sems.at[i]) for i in range(lines.shape[0])]


def middle_kernel(limit, chunk, counts, src, dst, w, back, got_prev, got_next, part, hid, w2, grad_two, grad, back_prev, back_next, slots, n_back, returned, w2_pad, slot_s, slot_sems, src_s, dst_s, sems, *accs):
    edges = Edges(counts[0], counts[1], w, (src, dst), (src_s, dst_s), sems)
    edges.fetch()
    side = slots.shape[0] // 2
    half = (got_prev.shape[0] - side) // 3
    for k, got in enumerate((got_prev, got_next)):
        slot = got[3 * half :, :].astype(jnp.int32)
        slots[k * side : (k + 1) * side, :] = jnp.maximum(slot, 0) + (1 - k) * side * LANES
        n_back[k] = jnp.sum((slot >= 0).astype(F32)).astype(jnp.int32)
    w2_b = padded(w2, w2_pad)
    unpack_rows(got_prev, returned, 0, half)
    unpack_rows(got_next, returned, 2 * half, half)
    fetch = fetch_lines(slots, slot_s, slot_sems)
    for c in fetch:
        c.start()
    copy_in(accs[0], part)
    for a in accs[1:]:
        fill_zero(a)
    for c in fetch:
        c.wait()
    take_returns(back, slot_s, n_back, part, returned.at[pl.ds(0, 4 * half)], returned.at[pl.ds(4 * half, 4 * half)], accs)
    grad_two[...] = jnp.zeros_like(grad_two)

    @pl.loop(0, hid.shape[0], step=STEP)
    def _(i):
        even, odd = halves(accs, i, STEP)
        d_tab = stack_lanes([even, odd]).astype(BF16)
        h = hid[pl.ds(i, STEP), :]
        grad_two[...] += dot(d_tab, h, ROWS_A)
        d_hid = dot(d_tab, w2_b)
        d_pre = jnp.where(h > 0, d_hid, 0.0)
        put_halves(grad, i, STEP, d_pre[:, :LANES], d_pre[:, LANES:])

    backward_halo(limit, chunk, edges, src_s, dst_s, grad, back_prev, back_next, accs, True)


def last_kernel(back, n_back, slots, got_prev, got_next, part, x, grad_one, slot_s, slot_sems, *accs):
    fetch = fetch_lines(slots, slot_s, slot_sems)
    for c in fetch:
        c.start()
    copy_in(accs[0], part)
    for a in accs[1:]:
        fill_zero(a)
    for c in fetch:
        c.wait()
    take_returns(back, slot_s, n_back, part, got_prev, got_next, accs)
    grad_one[...] = jnp.zeros_like(grad_one)

    @pl.loop(0, x.shape[0], step=STEP)
    def _(i):
        even, odd = halves(accs, i, STEP)
        d_tab = stack_lanes([even, odd]).astype(BF16)
        grad_one[...] += dot(x[pl.ds(i, STEP), :], d_tab, ROWS_A)


def call(body, name, outs, ins, scratch, out_specs=None, collective=None, vmem=14):
    extra = {} if collective is None else dict(collective_id=collective, has_side_effects=True)
    return pl.pallas_call(
        body, name=name, out_shape=outs, in_specs=ins, out_specs=out_specs or jax.tree.map(lambda _: VMEM, outs),
        scratch_shapes=[pltpu.VMEM(s, F32) if isinstance(s, tuple) else s for s in scratch],
        compiler_params=pltpu.CompilerParams(vmem_limit_bytes=vmem * 2**20, **extra),
        cost_estimate=pl.CostEstimate(flops=10**10, bytes_accessed=10**7, transcendentals=0),
    )


def solution(mesh):
    num_dev = mesh.shape[AXIS]
    to_next = [(d, (d + 1) % num_dev) for d in range(num_dev)]
    to_prev = [(d, (d - 1) % num_dev) for d in range(num_dev)]

    def step(x, w_one, w_two, send, edge_src, edge_dst, edge_w, labels, mask):
        rows, halo, edges, classes = x.shape[0], send.shape[1], edge_src.shape[0], w_two.shape[1]
        tab, half, w2_pad = (2 * rows, LANES), (2 * halo, LANES), (2 * LANES, 2 * LANES)
        sds = jax.ShapeDtypeStruct
        tab_f = sds(tab, F32)
        half_b, pack_b = sds((halo, 2 * LANES), BF16), sds((3 * halo // 2, LANES), BF16)
        wide_b = pltpu.VMEM((rows, 2 * LANES), BF16)
        one = sds(TILE, F32)
        dma = pltpu.SemaphoreType.DMA
        chunk_l, chunk_h = 64, 32
        lines = edges // LANES
        slots = lines + 8
        side = halo // LANES
        w2 = w_two.T
        mask = mask.reshape(-1, LANES)
        labels = labels.reshape(-1, LANES)
        lined = [a.reshape(lines, LANES) for a in (edge_src, edge_dst, edge_w)]
        ints = sds((slots, LANES), jnp.int32)
        sided = sds((2 * side, LANES), F32)
        tab_one, tab_b, src, dst, w_lines, used, counts, count, need = call(
            functools.partial(prep_kernel, num_dev, PREP_CHUNK, rows), "prep",
            [tab_f, sds((rows, 2 * LANES), BF16), ints, ints, sds((slots, LANES), F32), sided, sds((2,), jnp.int32), one, sds((1,), jnp.int32)],
            [VMEM] * 6,
            [(6 * slots, LANES), (6 * lines, LANES), pltpu.VMEM((4 * lines, LANES), jnp.int32), sided.shape, (2, LANES), (num_dev - 1, 2, LANES)]
            + [dma((num_dev - 1,))] * 2,
            out_specs=[VMEM] * 6 + [SMEM, VMEM, SMEM], vmem=60, collective=0,
        )(*lined, mask, x, w_one)

        def run(limit):
            compact = limit < halo
            pack_f, half_f = sds((3 * limit // 2 + side, LANES), F32), sds((2 * limit, LANES), F32)
            list_s = [pltpu.SMEM((halo,), jnp.int32), dma((side,))]
            to_p, to_n, w, src_back, lists = call(
                functools.partial(first_kernel, compact, halo), "first", [half_b, half_b, sds((slots * LANES, LANES), F32), ints, sided],
                [VMEM] * 3 + [SMEM] + [VMEM] * 3, [half] + list_s, vmem=8,
            )(tab_one, tab_b, send, counts, src, w_lines, used)
            from_prev = lax.ppermute(to_n, AXIS, to_next)
            from_next = lax.ppermute(to_p, AXIS, to_prev)
            flat, flat_dst, flat_back = src.reshape(-1), dst.reshape(-1), src_back.reshape(-1)

            four = [tab] * 4
            walk = [SMEM, ANY, ANY, VMEM]
            index = pltpu.SMEM((slots * LANES,), jnp.int32)
            walk_s = lambda n: [index] * n + [dma((n, slots * LANES // SEGMENT))]
            slot_s = [pltpu.SMEM((2 * halo,), jnp.int32), dma((2 * side,))]
            local, local_back = (
                call(functools.partial(local_kernel, chunk_l, back), "local_edges", tab_f, walk + [VMEM], walk_s(2) + four)
                for back in (False, True)
            )
            part = local(counts, flat, flat_dst, w, tab_one)
            hid, tab_two, to_p, to_n, back = call(
                functools.partial(hidden_kernel, chunk_h), "hidden",
                [sds((rows, 2 * LANES), BF16), tab_f, pack_b, pack_b, sds((2 * side, LANES), jnp.int32)],
                walk + [VMEM] * 5, [tab, wide_b, w2_pad, half] + list_s + walk_s(2) + four,
            )(counts, flat, flat_dst, w, send, from_prev, from_next, part, w2)
            from_prev = lax.ppermute(to_n, AXIS, to_next)
            from_next = lax.ppermute(to_p, AXIS, to_prev)
            back = back.reshape(-1)
            part = local(counts, flat, flat_dst, w, tab_two)
            loss, grad, to_p, to_n = call(
                functools.partial(loss_kernel, limit, 4, chunk_h, classes), "loss", [one, tab_f, pack_f, pack_f],
                walk + [ANY] + [VMEM] * 7, [tab] + walk_s(3) + four,
            )(counts, flat, flat_dst, w, flat_back, lists, count, from_prev, from_next, part, labels, mask)
            got_prev = lax.ppermute(to_p, AXIS, to_prev)
            got_next = lax.ppermute(to_n, AXIS, to_next)
            part = local_back(counts, flat, flat_dst, w, grad)
            grad_two, grad, to_p, to_n, slot, n_back = call(
                functools.partial(middle_kernel, limit, chunk_h), "middle",
                [sds(w2_pad, F32), tab_f, half_f, half_f, sds((2 * side, LANES), jnp.int32), sds((2,), jnp.int32)],
                walk + [SMEM] + [VMEM] * 5, [(4 * limit, LANES), w2_pad] + slot_s + walk_s(2) + four, out_specs=[VMEM] * 5 + [SMEM],
            )(counts, flat_back, flat_dst, w, back, got_prev, got_next, part, hid, w2)
            got_prev = lax.ppermute(to_p, AXIS, to_prev)
            got_next = lax.ppermute(to_n, AXIS, to_next)
            part = local_back(counts, flat, flat_dst, w, grad)
            grad_one = call(
                last_kernel, "last", sds((x.shape[1], 2 * LANES), F32), [SMEM, SMEM, ANY] + [VMEM] * 4, slot_s + four
            )(back, n_back, slot, got_prev, got_next, part, x)
            return grad_one, grad_two, loss

        limits = [halo // 32 * part for part in (16, 19, 32)]
        need = need.reshape(())
        choice = sum((need > limit).astype(jnp.int32) for limit in limits[:-1])
        grad_one, grad_two, loss = lax.switch(choice, [functools.partial(run, limit) for limit in limits])
        unit = SUB * num_dev
        lines = 2 * (x.shape[1] + -(-classes // SUB) * SUB) + SUB
        lines = -(-lines // unit) * unit
        grad_one, grad_two, mean = call(
            functools.partial(reduce_kernel, num_dev), "reduce", [sds(grad_one.shape, F32), sds((classes, 2 * LANES), F32), sds((1, 1), F32)],
            [VMEM] * 4, [(lines, LANES), (lines, LANES), (lines // 2, LANES), (num_dev // 2 - 1, lines // num_dev, LANES), dma((2, 2 * num_dev))],
            collective=1, vmem=8,
        )(grad_one, grad_two, loss, count)
        return mean.reshape(()), grad_one, grad_two.T

    row = P(AXIS)
    return jax.shard_map(
        step, mesh=mesh, in_specs=(row, P(), P(), row, row, row, row, row, row), out_specs=(P(), P(), P()), check_vma=False
    )
```

profile of v0, /device:TPU:0, one launch (start us, length us, event | category | flops | bytes accessed | tf_op | source)
XLA Modules:
  0.0 115.5 jit_solution(2511841269995987916)
XLA Ops:
  0.6 0.0 copy-start
  0.6 0.0 copy-start.1
  0.7 0.0 copy-start.2
  0.7 0.0 copy-start.3
  0.7 0.0 copy-start.4
  0.7 11.5 %prep.1 = (f32[4096,128]{1,0:T(8,128)S(1)}, bf16[2048,256]{1,0:T(8,128)(2,1)S(1)}, s32[72,128]{1,0:T(8,128)S(1)}, s32[72,128]{1,0:T(8,128)S(1)}, f32[72,128]{1,0...) custom-call(s32[64,128]{1,0:T(8,128)} %bitcast.37, ...), custom_call_target="tpu_custom_call" | custom-call | flops 10000000000 | bytes 10000000 | tf_op jit(solution)/shard_map/prep/pallas_call | solution.py:672
  13.3 0.0 copy-done
  13.3 0.0 copy-done.1
  13.3 0.0 copy-done.2
  13.3 0.0 copy-done.3
  13.3 0.0 copy-done.4
  13.3 84.7 %conditional.1 = (f32[128,256]{1,0:T(8,128)S(1)}, f32[256,256]{1,0:T(8,128)S(1)}, f32[8,128]{1,0:T(8,128)S(1)}) conditional(s32[]{:T(128)} %bitcast.16, (s32[72,128]{1,0:T(8,128)S(1)}, s32[72,128]{1,0:T(8,128)S(1)}, f32[4096,128]{1,0:T(8,128)S(1)}, bf16[2048,256]{1,0:T(8,128)(2,1)S(1)}, s32[2,1024]{1,0:T(2,128)S(1)}, ...), branch_computations={%region_0.0_spmd, %region_1.0_spmd, %region_2.0_spmd} | conditional | flops 89999998976 | bytes 112053208 | solution.py:735
  13.3 4.2 %first.3 = (bf16[1024,256]{1,0:T(8,128)(2,1)S(1)}, bf16[1024,256]{1,0:T(8,128)(2,1)S(1)}, f32[9216,128]{1,0:T(8,128)S(1)}, s32[72,128]{1,0:T(8,128)S(1)}, f32[16,128]{1,0:T(8,128)S(1)}) custom-call(f32[4096,128]{1,0:T(8,128)S(1)} %get-tuple-element.81.tab.table, bf16[2048,256]{1,0:T(8,128)(2,1)S(1)} %get-tuple-element.82.tab_b, ...), custom_call_target="tpu_custom_call" | custom-call | flops 10000000000 | bytes 10000000 | tf_op jit(solution)/shard_map/cond/branch_0_fun/first/pallas_call | solution.py:685
  17.6 0.4 collective-permute-start
  17.9 3.2 %collective-permute-start.1 = (bf16[1024,256]{1,0:T(8,128)(2,1)S(1)}, bf16[1024,256]{1,0:T(8,128)(2,1)S(1)}, u32[]{:S(2)}, u32[]{:S(2)}) collective-permute-start(bf16[1024,256]{1,0:T(8,128)(2,1)S(1)} %get-tuple-element.88), channel_id=1, source_target_pairs={{0,15},{1,0},{2,1},{3,2},{4,3},{5,4},{6,5},{7,6},{8,7},{9,8},{10,9... | collective-permute-start | bytes 1572872 | tf_op jit(solution)/shard_map/cond/branch_0_fun/ppermute | solution.py:690
  21.2 11.3 %local_edges.12.part = f32[4096,128]{1,0:T(8,128)S(1)} custom-call(s32[2]{0:T(128)S(1)} %get-tuple-element.78.counts, s32[9216]{0:T(1024)S(1)} %bitcast.47, s32[9216]{0:T(1024)S(1)} %bitcast.65, f32[9216,128]{1,0:T(8,128)S(1)} %get-tuple-element.86.w, f32[4096,128]{1,0:T(8,128)S(1)} %get-tuple-element.81.tab.table), custom_call_target="tpu_custom_call" | custom-call | flops 10000000000 | bytes 10000000 | tf_op jit(solution)/shard_map/cond/branch_0_fun/local_edges/pallas_call | solution.py:702
  32.5 0.4 collective-permute-done.from_prev
  32.9 0.0 collective-permute-done.1.from_next
  32.9 6.2 %hidden.3 = (bf16[2048,256]{1,0:T(8,128)(2,1)S(1)}, f32[4096,128]{1,0:T(8,128)S(1)}, bf16[1536,128]{1,0:T(8,128)(2,1)S(1)}, bf16[1536,128]{1,0:T(8,128)(2,1)S(1)}, s32[16,128]{1,0:T(8,128)S(1)}) custom-call(s32[2]{0:T(128)S(1)} %get-tuple-element.78.counts, s32[9216]{0:T(1024)S(1)} %bitcast.48, s32[9216]{0:T(1024)S(1)} %bitcast.66, ...), custom_call_target="tpu_custom_call" | custom-call | flops 10000000000 | bytes 10000000 | tf_op jit(solution)/shard_map/cond/branch_0_fun/hidden/pallas_call | solution.py:703
  39.2 0.1 collective-permute-start.2
  39.2 3.5 %collective-permute-start.3 = (bf16[1536,128]{1,0:T(8,128)(2,1)S(1)}, bf16[1536,128]{1,0:T(8,128)(2,1)S(1)}, u32[]{:S(2)}, u32[]{:S(2)}) collective-permute-start(bf16[1536,128]{1,0:T(8,128)(2,1)S(1)} %get-tuple-element.95), channel_id=1, source_target_pairs={{0,15},{1,0},{2,1},{3,2},{4,3},{5,4},{6,5},{7,6},{8,7},{9,8},{10,9... | collective-permute-start | bytes 1179656 | tf_op jit(solution)/shard_map/cond/branch_0_fun/ppermute | solution.py:709
  42.8 11.3 %local_edges.13.part = f32[4096,128]{1,0:T(8,128)S(1)} custom-call(s32[2]{0:T(128)S(1)} %get-tuple-element.78.counts, s32[9216]{0:T(1024)S(1)} %bitcast.49, s32[9216]{0:T(1024)S(1)} %bitcast.67, f32[9216,128]{1,0:T(8,128)S(1)} %get-tuple-element.86.w, f32[4096,128]{1,0:T(8,128)S(1)} %get-tuple-element.96.table), custom_call_target="tpu_custom_call" | custom-call | flops 10000000000 | bytes 10000000 | tf_op jit(solution)/shard_map/cond/branch_0_fun/local_edges/pallas_call | solution.py:711
  54.1 0.0 collective-permute-done.2.from_prev
  54.1 0.0 collective-permute-done.3.from_next
  54.1 6.2 %loss.3 = (f32[8,128]{1,0:T(8,128)S(1)}, f32[4096,128]{1,0:T(8,128)S(1)}, f32[776,128]{1,0:T(8,128)S(1)}, f32[776,128]{1,0:T(8,128)S(1)}) custom-call(s32[2]{0:T(128)S(1)} %get-tuple-element.78.counts, s32[9216]{0:T(1024)S(1)} %bitcast.50, s32[9216]{0:T(1024)S(1)} %bitcast.68, f32[9216,128]{1,0:T(8,128)S(1)} %get-tuple-element.86.w, s32[9216]{0:T(1024)S(1)} %bitcast.22, ...), custom_call_target="tpu_custom_call" | custom-call | flops 10000000000 | bytes 10000000 | tf_op jit(solution)/shard_map/cond/branch_0_fun/loss/pallas_call | solution.py:712
  60.3 1.1 collective-permute-start.4
  61.4 0.0 collective-permute-start.5
  61.4 11.3 %local_edges.14.part = f32[4096,128]{1,0:T(8,128)S(1)} custom-call(s32[2]{0:T(128)S(1)} %get-tuple-element.78.counts, s32[9216]{0:T(1024)S(1)} %bitcast.51, s32[9216]{0:T(1024)S(1)} %bitcast.69, f32[9216,128]{1,0:T(8,128)S(1)} %get-tuple-element.86.w, f32[4096,128]{1,0:T(8,128)S(1)} %get-tuple-element.101.table), custom_call_target="tpu_custom_call" | custom-call | flops 10000000000 | bytes 10000000 | tf_op jit(solution)/shard_map/cond/branch_0_fun/local_edges/pallas_call | solution.py:718
  72.8 0.0 collective-permute-done.4.got_prev
  72.8 0.0 collective-permute-done.5.got_next
  72.8 6.2 %middle.3 = (f32[256,256]{1,0:T(8,128)S(1)}, f32[4096,128]{1,0:T(8,128)S(1)}, f32[1024,128]{1,0:T(8,128)S(1)}, f32[1024,128]{1,0:T(8,128)S(1)}, s32[16,128]{1,0:T(8,128)S(1)}, /*index=5*/s32[2]{0:T(128)S(1)}) custom-call(s32[2]{0:T(128)S(1)} %get-tuple-element.78.counts, s32[9216]{0:T(1024)S(1)} %bitcast.23, s32[9216]{0:T(1024)S(1)} %bitcast.70, ...), custom_call_target="tpu_custom_call" | custom-call | flops 10000000000 | bytes 10000000 | tf_op jit(solution)/shard_map/cond/branch_0_fun/middle/pallas_call | solution.py:719
  79.1 4.0 %collective-permute-start.6 = (f32[1024,128]{1,0:T(8,128)S(1)}, f32[1024,128]{1,0:T(8,128)S(1)}, u32[]{:S(2)}, u32[]{:S(2)}) collective-permute-start(f32[1024,128]{1,0:T(8,128)S(1)} %get-tuple-element.105), channel_id=1, source_target_pairs={{0,15},{1,0},{2,1},{3,2},{4,3},{5,4},{6,5},{7,6},{8,7},{9,8},{10,9... | collective-permute-start | bytes 1572872 | tf_op jit(solution)/shard_map/cond/branch_0_fun/ppermute | solution.py:724
  83.0 0.0 collective-permute-start.7
  83.0 11.3 %local_edges.15.part = f32[4096,128]{1,0:T(8,128)S(1)} custom-call(s32[2]{0:T(128)S(1)} %get-tuple-element.78.counts, s32[9216]{0:T(1024)S(1)} %bitcast.52, s32[9216]{0:T(1024)S(1)} %bitcast.71, f32[9216,128]{1,0:T(8,128)S(1)} %get-tuple-element.86.w, f32[4096,128]{1,0:T(8,128)S(1)} %get-tuple-element.107.table), custom_call_target="tpu_custom_call" | custom-call | flops 10000000000 | bytes 10000000 | tf_op jit(solution)/shard_map/cond/branch_0_fun/local_edges/pallas_call | solution.py:726
  94.4 0.0 collective-permute-done.6.got_prev
  94.4 0.0 collective-permute-done.7.got_next
  94.4 3.4 %last.3 = f32[128,256]{1,0:T(8,128)S(1)} custom-call(s32[2048]{0:T(1024)S(1)} %bitcast.29, s32[2]{0:T(128)S(1)} %get-tuple-element.103.n_back, s32[16,128]{1,0:T(8,128)S(1)} %get-tuple-element.104.slots, f32[1024,128]{1,0:T(8,128)S(1)} %collective-permute-done.6.got_prev, f32[1024,128]{1,0:T(8,128)S(1)} %collective-permute-done.7.got_next, ...), custom_call_target="tpu_custom_call" | custom-call | flops 10000000000 | bytes 10000000 | tf_op jit(solution)/shard_map/cond/branch_0_fun/last/pallas_call | solution.py:727
  98.1 14.4 %reduce.1 = (f32[128,256]{1,0:T(8,128)S(1)}, f32[172,256]{1,0:T(8,128)S(1)}, f32[1,1]{1,0:T(1,128)}) custom-call(f32[128,256]{1,0:T(8,128)S(1)} %get-tuple-element.204.one, f32[256,256]{1,0:T(8,128)S(1)} %get-tuple-element.205.two, f32[8,128]{1,0:T(8,128)S(1)} %get-tuple-element.206.loss, f32[8,128]{1,0:T(8,128)S(1)} %get-tuple-element.203.count), custom_call_target="tpu_custom_call" | custom-call | flops 10000000000 | bytes 10000000 | tf_op jit(solution)/shard_map/reduce/pallas_call | solution.py:739
  113.0 0.7 copy.25
  113.7 0.7 copy.26
Async XLA Ops:
  0.6 12.6 %copy-start = (bf16[2048,128]{1,0:T(8,128)(2,1)S(1)}, bf16[2048,128]{1,0:T(8,128)(2,1)}, u32[]{:S(2)}) copy-start(bf16[2048,128]{1,0:T(8,128)(2,1)} %x.1) | copy-start | bytes 1572868
  0.6 12.6 %copy-start.1 = (f32[256,172]{0,1:T(8,128)S(1)}, f32[256,172]{0,1:T(8,128)}, u32[]{:S(2)}) copy-start(f32[256,172]{0,1:T(8,128)} %param.14) | copy-start | bytes 528388
  0.7 12.6 %copy-start.2 = (s32[2048]{0:T(1024)S(1)}, s32[2048]{0:T(1024)}, u32[]{:S(2)}) copy-start(s32[2048]{0:T(1024)} %param.20) | copy-start | bytes 24580
  0.7 12.6 %copy-start.3 = (s32[2,1024]{1,0:T(2,128)S(1)}, s32[2,1024]{1,0:T(2,128)}, u32[]{:S(2)}) copy-start(s32[2,1024]{1,0:T(2,128)} %param.15) | copy-start | bytes 24580
  0.7 12.6 %copy-start.4 = (s32[2048]{0:T(1024)S(1)}, s32[2048]{0:T(1024)}, u32[]{:S(2)}) copy-start(s32[2048]{0:T(1024)} %param.19) | copy-start | bytes 24580
  17.6 15.4 %collective-permute-start = (bf16[1024,256]{1,0:T(8,128)(2,1)S(1)}, bf16[1024,256]{1,0:T(8,128)(2,1)S(1)}, u32[]{:S(2)}, u32[]{:S(2)}) collective-permute-start(bf16[1024,256]{1,0:T(8,128)(2,1)S(1)} %get-tuple-element.87), channel_id=1, source_target_pairs={{0,1},{1,2},{2,3},{3,4},{4,5},{5,6},{6,7},{7,8},{8,9},{9,10},{10,1... | collective-permute-start | bytes 1572872 | tf_op jit(solution)/shard_map/cond/branch_0_fun/ppermute | solution.py:689
  17.9 15.0 %collective-permute-start.1 = (bf16[1024,256]{1,0:T(8,128)(2,1)S(1)}, bf16[1024,256]{1,0:T(8,128)(2,1)S(1)}, u32[]{:S(2)}, u32[]{:S(2)}) collective-permute-start(bf16[1024,256]{1,0:T(8,128)(2,1)S(1)} %get-tuple-element.88), channel_id=1, source_target_pairs={{0,15},{1,0},{2,1},{3,2},{4,3},{5,4},{6,5},{7,6},{8,7},{9,8},{10,9... | collective-permute-start | bytes 1572872 | tf_op jit(solution)/shard_map/cond/branch_0_fun/ppermute | solution.py:690
  39.2 14.9 %collective-permute-start.2 = (bf16[1536,128]{1,0:T(8,128)(2,1)S(1)}, bf16[1536,128]{1,0:T(8,128)(2,1)S(1)}, u32[]{:S(2)}, u32[]{:S(2)}) collective-permute-start(bf16[1536,128]{1,0:T(8,128)(2,1)S(1)} %get-tuple-element.94), channel_id=1, source_target_pairs={{0,1},{1,2},{2,3},{3,4},{4,5},{5,6},{6,7},{7,8},{8,9},{9,10},{10,1... | collective-permute-start | bytes 1179656 | tf_op jit(solution)/shard_map/cond/branch_0_fun/ppermute | solution.py:708
  39.2 14.9 %collective-permute-start.3 = (bf16[1536,128]{1,0:T(8,128)(2,1)S(1)}, bf16[1536,128]{1,0:T(8,128)(2,1)S(1)}, u32[]{:S(2)}, u32[]{:S(2)}) collective-permute-start(bf16[1536,128]{1,0:T(8,128)(2,1)S(1)} %get-tuple-element.95), channel_id=1, source_target_pairs={{0,15},{1,0},{2,1},{3,2},{4,3},{5,4},{6,5},{7,6},{8,7},{9,8},{10,9... | collective-permute-start | bytes 1179656 | tf_op jit(solution)/shard_map/cond/branch_0_fun/ppermute | solution.py:709
  60.3 12.5 %collective-permute-start.4 = (f32[776,128]{1,0:T(8,128)S(1)}, f32[776,128]{1,0:T(8,128)S(1)}, u32[]{:S(2)}, u32[]{:S(2)}) collective-permute-start(f32[776,128]{1,0:T(8,128)S(1)} %get-tuple-element.99), channel_id=1, source_target_pairs={{0,15},{1,0},{2,1},{3,2},{4,3},{5,4},{6,5},{7,6},{8,7},{9,8},{10,9... | collective-permute-start | bytes 1191944 | tf_op jit(solution)/shard_map/cond/branch_0_fun/ppermute | solution.py:716
  61.4 11.4 %collective-permute-start.5 = (f32[776,128]{1,0:T(8,128)S(1)}, f32[776,128]{1,0:T(8,128)S(1)}, u32[]{:S(2)}, u32[]{:S(2)}) collective-permute-start(f32[776,128]{1,0:T(8,128)S(1)} %get-tuple-element.100), channel_id=1, source_target_pairs={{0,1},{1,2},{2,3},{3,4},{4,5},{5,6},{6,7},{7,8},{8,9},{9,10},{10,1... | collective-permute-start | bytes 1191944 | tf_op jit(solution)/shard_map/cond/branch_0_fun/ppermute | solution.py:717
  79.1 15.3 %collective-permute-start.6 = (f32[1024,128]{1,0:T(8,128)S(1)}, f32[1024,128]{1,0:T(8,128)S(1)}, u32[]{:S(2)}, u32[]{:S(2)}) collective-permute-start(f32[1024,128]{1,0:T(8,128)S(1)} %get-tuple-element.105), channel_id=1, source_target_pairs={{0,15},{1,0},{2,1},{3,2},{4,3},{5,4},{6,5},{7,6},{8,7},{9,8},{10,9... | collective-permute-start | bytes 1572872 | tf_op jit(solution)/shard_map/cond/branch_0_fun/ppermute | solution.py:724
  83.0 11.4 %collective-permute-start.7 = (f32[1024,128]{1,0:T(8,128)S(1)}, f32[1024,128]{1,0:T(8,128)S(1)}, u32[]{:S(2)}, u32[]{:S(2)}) collective-permute-start(f32[1024,128]{1,0:T(8,128)S(1)} %get-tuple-element.106), channel_id=1, source_target_pairs={{0,1},{1,2},{2,3},{3,4},{4,5},{5,6},{6,7},{7,8},{8,9},{9,10},{10,1... | collective-permute-start | bytes 1572872 | tf_op jit(solution)/shard_map/cond/branch_0_fun/ppermute | solution.py:725
where the time goes:
time: 118 us; the launch traced here: 115 us
  Pallas kernels  97.5 us (83%)
  starting transfers between devices  12.3 us (10%)
  between operations  3.51 us (3%)
  local copies, waits for them, and re-layouts  1.35 us (1%)
    pallas_call x2, Pallas kernels, run(): part = local_back(counts, flat, flat_dst, w, grad)  22.7 us
    pallas_call x1, Pallas kernels, step(): call(functools.partial(reduce_kernel, num_dev), 'reduce', [sds(grad_one.s...  14.4 us
    pallas_call x1, Pallas kernels, step(): call(functools.partial(prep_kernel, num_dev, PREP_CHUNK, rows), 'prep', [...  11.5 us
    pallas_call x1, Pallas kernels, run(): part = local(counts, flat, flat_dst, w, tab_one)  11.3 us
    pallas_call x1, Pallas kernels, run(): part = local(counts, flat, flat_dst, w, tab_two)  11.3 us
    ppermute x2, starting transfers between devices, run(): from_next = lax.ppermute(to_p, AXIS, to_prev)  6.75 us
    pallas_call x1, Pallas kernels, run(): call(functools.partial(middle_kernel, limit, chunk_h), 'middle', [sds(w2_...  6.25 us
    pallas_call x1, Pallas kernels, run(): call(functools.partial(hidden_kernel, chunk_h), 'hidden', [sds((rows, 2 *...  6.23 us
  transfers between devices with their start and end apart: 8, of which 1 were waited for; matrix products, arithmetic and copies ran while one was open for 0% of the time, Pallas kernels for 39%

commit v1 on v0

--- a/solution.py
+++ b/solution.py
@@ -729,7 +729,7 @@
             )(back, n_back, slot, got_prev, got_next, part, x)
             return grad_one, grad_two, loss
 
-        limits = [halo // 32 * part for part in (16, 19, 32)]
+        limits = [halo // 32 * part for part in (15, 17, 19, 32)]
         need = need.reshape(())
         choice = sum((need > limit).astype(jnp.int32) for limit in limits[:-1])
         grad_one, grad_two, loss = lax.switch(choice, [functools.partial(run, limit) for limit in limits])

time: 118 us -> 120 us (1.017); the launches traced: 115 us -> 121 us
  Pallas kernels: 97.5 us -> 103 us
  starting transfers between devices: 12.3 us -> 10.1 us
    ppermute x2, starting transfers between devices: 5.11 us -> 2.46 us  [run(): got_prev = lax.ppermute(to_p, AXIS, to_prev)]
    ppermute x2, waiting for transfers between devices: 0.01 us -> 1.61 us  [run(): got_prev = lax.ppermute(to_p, AXIS, to_prev)]
    pallas_call x1, Pallas kernels: 6.16 us -> 7.36 us  [run(): call(functools.partial(loss_kernel, limit, 4, chunk_h, classes), 'loss',...]
where the time goes in v1:
time: 120 us; the launch traced here: 121 us
  Pallas kernels  103 us (86%)
  starting transfers between devices  10.1 us (8%)
  between operations  4.56 us (4%)
  waiting for transfers between devices  1.63 us (1%)
  local copies, waits for them, and re-layouts  1.35 us (1%)
    pallas_call x2, Pallas kernels, run(): part = local_back(counts, flat, flat_dst, w, grad)  23.4 us
    pallas_call x1, Pallas kernels, step(): call(functools.partial(reduce_kernel, num_dev), 'reduce', [sds(grad_one.s...  15.2 us
    pallas_call x1, Pallas kernels, run(): part = local(counts, flat, flat_dst, w, tab_one)  11.7 us
    pallas_call x1, Pallas kernels, run(): part = local(counts, flat, flat_dst, w, tab_two)  11.7 us
    pallas_call x1, Pallas kernels, step(): call(functools.partial(prep_kernel, num_dev, PREP_CHUNK, rows), 'prep', [...  11.5 us
    pallas_call x1, Pallas kernels, run(): call(functools.partial(loss_kernel, limit, 4, chunk_h, classes), 'loss',...  7.36 us
    pallas_call x1, Pallas kernels, run(): call(functools.partial(middle_kernel, limit, chunk_h), 'middle', [sds(w2_...  7.34 us
    ppermute x2, starting transfers between devices, run(): from_next = lax.ppermute(to_p, AXIS, to_prev)  6.95 us
  transfers between devices with their start and end apart: 8, of which 1 were waited for; matrix products, arithmetic and copies ran while one was open for 0% of the time, Pallas kernels for 39%

profile of v1, /device:TPU:0, one launch (start us, length us, event | category | flops | bytes accessed | tf_op | source)
XLA Modules:
  0.0 120.8 jit_solution(7506266953690778140)
XLA Ops:
  0.6 0.0 copy-start
  0.6 0.0 copy-start.1
  0.7 0.0 copy-start.2
  0.7 0.0 copy-start.3
  0.7 0.0 copy-start.4
  0.7 11.5 %prep.1 = (f32[4096,128]{1,0:T(8,128)S(1)}, bf16[2048,256]{1,0:T(8,128)(2,1)S(1)}, s32[72,128]{1,0:T(8,128)S(1)}, s32[72,128]{1,0:T(8,128)S(1)}, f32[72,128]{1,0...) custom-call(s32[64,128]{1,0:T(8,128)} %bitcast.46, ...), custom_call_target="tpu_custom_call" | custom-call | flops 10000000000 | bytes 10000000 | tf_op jit(solution)/shard_map/prep/pallas_call | solution.py:672
  14.2 0.0 copy-done
  14.2 0.0 copy-done.1
  14.2 0.0 copy-done.2
  14.2 0.0 copy-done.3
  14.2 0.0 copy-done.4
  14.2 88.2 %conditional.1 = (f32[128,256]{1,0:T(8,128)S(1)}, f32[256,256]{1,0:T(8,128)S(1)}, f32[8,128]{1,0:T(8,128)S(1)}) conditional(s32[]{:T(128)} %bitcast.20, (s32[72,128]{1,0:T(8,128)S(1)}, s32[72,128]{1,0:T(8,128)S(1)}, f32[4096,128]{1,0:T(8,128)S(1)}, bf16[2048,256]{1,0:T(8,128)(2,1)S(1)}, s32[2,1024]{1,0:T(2,128)S(1)}, ...), branch_computations={%region_0.0_spmd, %region_1.0_spmd, %region_2.0_spmd, %region_3.0_... | conditional | flops 89999998976 | bytes 112053208 | solution.py:735
  14.5 4.4 %first.6 = (bf16[1024,256]{1,0:T(8,128)(2,1)S(1)}, bf16[1024,256]{1,0:T(8,128)(2,1)S(1)}, f32[9216,128]{1,0:T(8,128)S(1)}, s32[72,128]{1,0:T(8,128)S(1)}, f32[16,128]{1,0:T(8,128)S(1)}) custom-call(f32[4096,128]{1,0:T(8,128)S(1)} %get-tuple-element.173.tab.table, bf16[2048,256]{1,0:T(8,128)(2,1)S(1)} %get-tuple-element.174.tab_b, ...), custom_call_target="tpu_custom_call" | custom-call | flops 10000000000 | bytes 10000000 | tf_op jit(solution)/shard_map/cond/branch_2_fun/first/pallas_call | solution.py:685
  18.9 0.2 collective-permute-start.16
  19.1 3.4 %collective-permute-start.17 = (bf16[1024,256]{1,0:T(8,128)(2,1)S(1)}, bf16[1024,256]{1,0:T(8,128)(2,1)S(1)}, u32[]{:S(2)}, u32[]{:S(2)}) collective-permute-start(bf16[1024,256]{1,0:T(8,128)(2,1)S(1)} %get-tuple-element.180), channel_id=1, source_target_pairs={{0,15},{1,0},{2,1},{3,2},{4,3},{5,4},{6,5},{7,6},{8,7},{9,8},{10,9... | collective-permute-start | bytes 1572872 | tf_op jit(solution)/shard_map/cond/branch_2_fun/ppermute | solution.py:690
  22.5 11.7 %local_edges.24.part = f32[4096,128]{1,0:T(8,128)S(1)} custom-call(s32[2]{0:T(128)S(1)} %get-tuple-element.170.counts, s32[9216]{0:T(1024)S(1)} %bitcast.70, s32[9216]{0:T(1024)S(1)} %bitcast.96, f32[9216,128]{1,0:T(8,128)S(1)} %get-tuple-element.178.w, f32[4096,128]{1,0:T(8,128)S(1)} %get-tuple-element.173.tab.table), custom_call_target="tpu_custom_call" | custom-call | flops 10000000000 | bytes 10000000 | tf_op jit(solution)/shard_map/cond/branch_2_fun/local_edges/pallas_call | solution.py:702
  34.2 0.0 collective-permute-done.16.from_prev
  34.2 0.0 collective-permute-done.17.from_next
  34.2 6.6 %hidden.6 = (bf16[2048,256]{1,0:T(8,128)(2,1)S(1)}, f32[4096,128]{1,0:T(8,128)S(1)}, bf16[1536,128]{1,0:T(8,128)(2,1)S(1)}, bf16[1536,128]{1,0:T(8,128)(2,1)S(1)}, s32[16,128]{1,0:T(8,128)S(1)}) custom-call(s32[2]{0:T(128)S(1)} %get-tuple-element.170.counts, s32[9216]{0:T(1024)S(1)} %bitcast.71, s32[9216]{0:T(1024)S(1)} %bitcast.97, ...), custom_call_target="tpu_custom_call" | custom-call | flops 10000000000 | bytes 10000000 | tf_op jit(solution)/shard_map/cond/branch_2_fun/hidden/pallas_call | solution.py:703
  40.8 0.1 collective-permute-start.18
  40.9 3.5 %collective-permute-start.19 = (bf16[1536,128]{1,0:T(8,128)(2,1)S(1)}, bf16[1536,128]{1,0:T(8,128)(2,1)S(1)}, u32[]{:S(2)}, u32[]{:S(2)}) collective-permute-start(bf16[1536,128]{1,0:T(8,128)(2,1)S(1)} %get-tuple-element.187), channel_id=1, source_target_pairs={{0,15},{1,0},{2,1},{3,2},{4,3},{5,4},{6,5},{7,6},{8,7},{9,8},{10,9... | collective-permute-start | bytes 1179656 | tf_op jit(solution)/shard_map/cond/branch_2_fun/ppermute | solution.py:709
  44.4 11.7 %local_edges.25.part = f32[4096,128]{1,0:T(8,128)S(1)} custom-call(s32[2]{0:T(128)S(1)} %get-tuple-element.170.counts, s32[9216]{0:T(1024)S(1)} %bitcast.72, s32[9216]{0:T(1024)S(1)} %bitcast.98, f32[9216,128]{1,0:T(8,128)S(1)} %get-tuple-element.178.w, f32[4096,128]{1,0:T(8,128)S(1)} %get-tuple-element.188.table), custom_call_target="tpu_custom_call" | custom-call | flops 10000000000 | bytes 10000000 | tf_op jit(solution)/shard_map/cond/branch_2_fun/local_edges/pallas_call | solution.py:711
  56.1 0.0 collective-permute-done.18.from_prev
  56.1 0.0 collective-permute-done.19.from_next
  56.1 7.4 %loss.6 = (f32[8,128]{1,0:T(8,128)S(1)}, f32[4096,128]{1,0:T(8,128)S(1)}, f32[920,128]{1,0:T(8,128)S(1)}, f32[920,128]{1,0:T(8,128)S(1)}) custom-call(s32[2]{0:T(128)S(1)} %get-tuple-element.170.counts, s32[9216]{0:T(1024)S(1)} %bitcast.73, s32[9216]{0:T(1024)S(1)} %bitcast.99, f32[9216,128]{1,0:T(8,128)S(1)} %get-tuple-element.178.w, s32[9216]{0:T(1024)S(1)} %bitcast.30, ...), custom_call_target="tpu_custom_call" | custom-call | flops 10000000000 | bytes 10000000 | tf_op jit(solution)/shard_map/cond/branch_2_fun/loss/pallas_call | solution.py:712
  63.5 0.1 collective-permute-start.20
  63.5 0.5 collective-permute-start.21
  64.0 11.7 %local_edges.26.part = f32[4096,128]{1,0:T(8,128)S(1)} custom-call(s32[2]{0:T(128)S(1)} %get-tuple-element.170.counts, s32[9216]{0:T(1024)S(1)} %bitcast.74, s32[9216]{0:T(1024)S(1)} %bitcast.100, f32[9216,128]{1,0:T(8,128)S(1)} %get-tuple-element.178.w, f32[4096,128]{1,0:T(8,128)S(1)} %get-tuple-element.193.table), custom_call_target="tpu_custom_call" | custom-call | flops 10000000000 | bytes 10000000 | tf_op jit(solution)/shard_map/cond/branch_2_fun/local_edges/pallas_call | solution.py:718
  75.7 0.0 collective-permute-done.20.got_prev
  75.8 0.0 collective-permute-done.21.got_next
  75.8 7.3 %middle.6 = (f32[256,256]{1,0:T(8,128)S(1)}, f32[4096,128]{1,0:T(8,128)S(1)}, f32[1216,128]{1,0:T(8,128)S(1)}, f32[1216,128]{1,0:T(8,128)S(1)}, s32[16,128]{1,0:T(8,128)S(1)}, /*index=5*/s32[2]{0:T(128)S(1)}) custom-call(s32[2]{0:T(128)S(1)} %get-tuple-element.170.counts, s32[9216]{0:T(1024)S(1)} %bitcast.31, s32[9216]{0:T(1024)S(1)} %bitcast.101, ...), custom_call_target="tpu_custom_call" | custom-call | flops 10000000000 | bytes 10000000 | tf_op jit(solution)/shard_map/cond/branch_2_fun/middle/pallas_call | solution.py:719
  83.1 2.4 %collective-permute-start.22 = (f32[1216,128]{1,0:T(8,128)S(1)}, f32[1216,128]{1,0:T(8,128)S(1)}, u32[]{:S(2)}, u32[]{:S(2)}) collective-permute-start(f32[1216,128]{1,0:T(8,128)S(1)} %get-tuple-element.197), channel_id=1, source_target_pairs={{0,15},{1,0},{2,1},{3,2},{4,3},{5,4},{6,5},{7,6},{8,7},{9,8},{10,9... | collective-permute-start | bytes 1867784 | tf_op jit(solution)/shard_map/cond/branch_2_fun/ppermute | solution.py:724
  85.5 0.0 collective-permute-start.23
  85.5 11.7 %local_edges.27.part = f32[4096,128]{1,0:T(8,128)S(1)} custom-call(s32[2]{0:T(128)S(1)} %get-tuple-element.170.counts, s32[9216]{0:T(1024)S(1)} %bitcast.75, s32[9216]{0:T(1024)S(1)} %bitcast.102, f32[9216,128]{1,0:T(8,128)S(1)} %get-tuple-element.178.w, f32[4096,128]{1,0:T(8,128)S(1)} %get-tuple-element.199.table), custom_call_target="tpu_custom_call" | custom-call | flops 10000000000 | bytes 10000000 | tf_op jit(solution)/shard_map/cond/branch_2_fun/local_edges/pallas_call | solution.py:726
  97.2 1.6 %collective-permute-done.22.got_prev = f32[1216,128]{1,0:T(8,128)S(1)} collective-permute-done((f32[1216,128]{1,0:T(8,128)S(1)}, f32[1216,128]{1,0:T(8,128)S(1)}, u32[]{:S(2)}, u32[]{:S(2)}) %collective-permute-start.22) | collective-permute-done | bytes 622624 | tf_op jit(solution)/shard_map/cond/branch_2_fun/ppermute | solution.py:724
  98.9 0.0 collective-permute-done.23.got_next
  98.9 3.5 %last.6 = f32[128,256]{1,0:T(8,128)S(1)} custom-call(s32[2048]{0:T(1024)S(1)} %bitcast.39, s32[2]{0:T(128)S(1)} %get-tuple-element.195.n_back, s32[16,128]{1,0:T(8,128)S(1)} %get-tuple-element.196.slots, f32[1216,128]{1,0:T(8,128)S(1)} %collective-permute-done.22.got_prev, f32[1216,128]{1,0:T(8,128)S(1)} %collective-permute-done.23.got_next, ...), custom_call_target="tpu_custom_call" | custom-call | flops 10000000000 | bytes 10000000 | tf_op jit(solution)/shard_map/cond/branch_2_fun/last/pallas_call | solution.py:727
  102.4 15.2 %reduce.1 = (f32[128,256]{1,0:T(8,128)S(1)}, f32[172,256]{1,0:T(8,128)S(1)}, f32[1,1]{1,0:T(1,128)}) custom-call(f32[128,256]{1,0:T(8,128)S(1)} %get-tuple-element.263.one, f32[256,256]{1,0:T(8,128)S(1)} %get-tuple-element.264.two, f32[8,128]{1,0:T(8,128)S(1)} %get-tuple-element.265.loss, f32[8,128]{1,0:T(8,128)S(1)} %get-tuple-element.262.count), custom_call_target="tpu_custom_call" | custom-call | flops 10000000000 | bytes 10000000 | tf_op jit(solution)/shard_map/reduce/pallas_call | solution.py:739
  118.3 0.7 copy.28
  119.0 0.7 copy.29
Async XLA Ops:
  0.6 13.6 %copy-start = (bf16[2048,128]{1,0:T(8,128)(2,1)S(1)}, bf16[2048,128]{1,0:T(8,128)(2,1)}, u32[]{:S(2)}) copy-start(bf16[2048,128]{1,0:T(8,128)(2,1)} %x.1) | copy-start | bytes 1572868
  0.6 13.6 %copy-start.1 = (f32[256,172]{0,1:T(8,128)S(1)}, f32[256,172]{0,1:T(8,128)}, u32[]{:S(2)}) copy-start(f32[256,172]{0,1:T(8,128)} %param.15) | copy-start | bytes 528388
  0.7 13.6 %copy-start.2 = (s32[2048]{0:T(1024)S(1)}, s32[2048]{0:T(1024)}, u32[]{:S(2)}) copy-start(s32[2048]{0:T(1024)} %param.21) | copy-start | bytes 24580
  0.7 13.6 %copy-start.3 = (s32[2,1024]{1,0:T(2,128)S(1)}, s32[2,1024]{1,0:T(2,128)}, u32[]{:S(2)}) copy-start(s32[2,1024]{1,0:T(2,128)} %param.16) | copy-start | bytes 24580
  0.7 13.6 %copy-start.4 = (s32[2048]{0:T(1024)S(1)}, s32[2048]{0:T(1024)}, u32[]{:S(2)}) copy-start(s32[2048]{0:T(1024)} %param.20) | copy-start | bytes 24580
  18.9 15.3 %collective-permute-start.16 = (bf16[1024,256]{1,0:T(8,128)(2,1)S(1)}, bf16[1024,256]{1,0:T(8,128)(2,1)S(1)}, u32[]{:S(2)}, u32[]{:S(2)}) collective-permute-start(bf16[1024,256]{1,0:T(8,128)(2,1)S(1)} %get-tuple-element.179), channel_id=1, source_target_pairs={{0,1},{1,2},{2,3},{3,4},{4,5},{5,6},{6,7},{7,8},{8,9},{9,10},{10,1... | collective-permute-start | bytes 1572872 | tf_op jit(solution)/shard_map/cond/branch_2_fun/ppermute | solution.py:689
  19.1 15.1 %collective-permute-start.17 = (bf16[1024,256]{1,0:T(8,128)(2,1)S(1)}, bf16[1024,256]{1,0:T(8,128)(2,1)S(1)}, u32[]{:S(2)}, u32[]{:S(2)}) collective-permute-start(bf16[1024,256]{1,0:T(8,128)(2,1)S(1)} %get-tuple-element.180), channel_id=1, source_target_pairs={{0,15},{1,0},{2,1},{3,2},{4,3},{5,4},{6,5},{7,6},{8,7},{9,8},{10,9... | collective-permute-start | bytes 1572872 | tf_op jit(solution)/shard_map/cond/branch_2_fun/ppermute | solution.py:690
  40.8 15.3 %collective-permute-start.18 = (bf16[1536,128]{1,0:T(8,128)(2,1)S(1)}, bf16[1536,128]{1,0:T(8,128)(2,1)S(1)}, u32[]{:S(2)}, u32[]{:S(2)}) collective-permute-start(bf16[1536,128]{1,0:T(8,128)(2,1)S(1)} %get-tuple-element.186), channel_id=1, source_target_pairs={{0,1},{1,2},{2,3},{3,4},{4,5},{5,6},{6,7},{7,8},{8,9},{9,10},{10,1... | collective-permute-start | bytes 1179656 | tf_op jit(solution)/shard_map/cond/branch_2_fun/ppermute | solution.py:708
  40.9 15.2 %collective-permute-start.19 = (bf16[1536,128]{1,0:T(8,128)(2,1)S(1)}, bf16[1536,128]{1,0:T(8,128)(2,1)S(1)}, u32[]{:S(2)}, u32[]{:S(2)}) collective-permute-start(bf16[1536,128]{1,0:T(8,128)(2,1)S(1)} %get-tuple-element.187), channel_id=1, source_target_pairs={{0,15},{1,0},{2,1},{3,2},{4,3},{5,4},{6,5},{7,6},{8,7},{9,8},{10,9... | collective-permute-start | bytes 1179656 | tf_op jit(solution)/shard_map/cond/branch_2_fun/ppermute | solution.py:709
  63.5 12.3 %collective-permute-start.20 = (f32[920,128]{1,0:T(8,128)S(1)}, f32[920,128]{1,0:T(8,128)S(1)}, u32[]{:S(2)}, u32[]{:S(2)}) collective-permute-start(f32[920,128]{1,0:T(8,128)S(1)} %get-tuple-element.191), channel_id=1, source_target_pairs={{0,15},{1,0},{2,1},{3,2},{4,3},{5,4},{6,5},{7,6},{8,7},{9,8},{10,9... | collective-permute-start | bytes 1413128 | tf_op jit(solution)/shard_map/cond/branch_2_fun/ppermute | solution.py:716
  63.5 12.2 %collective-permute-start.21 = (f32[920,128]{1,0:T(8,128)S(1)}, f32[920,128]{1,0:T(8,128)S(1)}, u32[]{:S(2)}, u32[]{:S(2)}) collective-permute-start(f32[920,128]{1,0:T(8,128)S(1)} %get-tuple-element.192), channel_id=1, source_target_pairs={{0,1},{1,2},{2,3},{3,4},{4,5},{5,6},{6,7},{7,8},{8,9},{9,10},{10,1... | collective-permute-start | bytes 1413128 | tf_op jit(solution)/shard_map/cond/branch_2_fun/ppermute | solution.py:717
  83.1 15.7 %collective-permute-start.22 = (f32[1216,128]{1,0:T(8,128)S(1)}, f32[1216,128]{1,0:T(8,128)S(1)}, u32[]{:S(2)}, u32[]{:S(2)}) collective-permute-start(f32[1216,128]{1,0:T(8,128)S(1)} %get-tuple-element.197), channel_id=1, source_target_pairs={{0,15},{1,0},{2,1},{3,2},{4,3},{5,4},{6,5},{7,6},{8,7},{9,8},{10,9... | collective-permute-start | bytes 1867784 | tf_op jit(solution)/shard_map/cond/branch_2_fun/ppermute | solution.py:724
  85.5 13.3 %collective-permute-start.23 = (f32[1216,128]{1,0:T(8,128)S(1)}, f32[1216,128]{1,0:T(8,128)S(1)}, u32[]{:S(2)}, u32[]{:S(2)}) collective-permute-start(f32[1216,128]{1,0:T(8,128)S(1)} %get-tuple-element.198), channel_id=1, source_target_pairs={{0,1},{1,2},{2,3},{3,4},{4,5},{5,6},{6,7},{7,8},{8,9},{9,10},{10,1... | collective-permute-start | bytes 1867784 | tf_op jit(solution)/shard_map/cond/branch_2_fun/ppermute | solution.py:725
